TPU v7x, 32 devices: a whole 2x2x4 slice. The times are simulated.
32 devices in a mesh: row: 4 (over x, core), col: 8 (over z, y).
Axes of the slice: x: 2, y: 2, z: 4, core: 2. Of those that a mesh axis runs over, the one named last changes fastest.
Arguments:
- tiles: bfloat16 [4, 8, 128, 128, 128], P('row', 'col')
- tile_row: int32 [4, 8, 128], P('row', 'col'), may hold values from 0 to 15, as said below
- tile_col: int32 [4, 8, 128], P('row', 'col'), may hold values from 0 to 15
- tile_count: int32 [4, 8], P('row', 'col'), may hold values from 1 to 128, as said below
- sinogram: float32 [4, 2048, 128], P('row', 'col')
Outputs:
- volume: float32 [8, 2048, 128], P('col', 'row')
- residual: float32 [4, 2048, 128], P('row', 'col')
Inputs may be any that keep to these rules, and one draw needn't show every extreme that they name: Within one block the pairs (tile_row, tile_col) of all 128 slots are distinct. Slots 0 to tile_count - 1 of a block are live, the rest are ignored; some block has all 128 slots live in every draw.
All inputs are finite; a program needn't handle non-finite values.
Results may differ from a plain program's by a relative error of at most 0.015.
Values may be sent and summed in bfloat16 or wider, within the bound.
A program may use at most 64 MiB of HBM per device.

v0:
```python
import jax
import jax.numpy as jnp
from jax import lax
from jax.sharding import PartitionSpec as P

RT = 16
VT = 16
ITERS = 4


def frame_squares(values):
    return jnp.sum(values * values, axis=(0, 1))


def forward_local(blocks, rows_index, cols_index, count, voxel_block):
    tile = blocks.shape[1]
    frames = voxel_block.shape[1]
    voxel_tiles = voxel_block.reshape(voxel_block.shape[0] // tile, tile, frames)
    picked = jnp.take(voxel_tiles, cols_index, axis=0)
    products = jnp.einsum("tij,tjk->tik", blocks, picked, preferred_element_type=jnp.float32)
    live = jnp.arange(blocks.shape[0], dtype=jnp.int32) < count
    select = (
        (rows_index[None, :] == jnp.arange(RT, dtype=jnp.int32)[:, None]) & live[None, :]
    ).astype(jnp.float32)
    summed = jnp.einsum("ut,tik->uik", select, products, precision=lax.Precision.HIGHEST)
    return summed.reshape(RT * tile, frames)


def backward_local(blocks, rows_index, cols_index, count, ray_block):
    tile = blocks.shape[1]
    frames = ray_block.shape[1]
    ray_tiles = ray_block.reshape(ray_block.shape[0] // tile, tile, frames)
    picked = jnp.take(ray_tiles, rows_index, axis=0)
    products = jnp.einsum("tji,tjk->tik", blocks, picked, preferred_element_type=jnp.float32)
    live = jnp.arange(blocks.shape[0], dtype=jnp.int32) < count
    select = (
        (cols_index[None, :] == jnp.arange(VT, dtype=jnp.int32)[:, None]) & live[None, :]
    ).astype(jnp.float32)
    summed = jnp.einsum("ut,tik->uik", select, products, precision=lax.Precision.HIGHEST)
    return summed.reshape(VT * tile, frames)


def local(tiles, tile_row, tile_col, tile_count, sinogram):
    blocks = tiles[0, 0]
    rows_index = tile_row[0, 0]
    cols_index = tile_col[0, 0]
    count = tile_count[0, 0]
    tile = blocks.shape[1]
    frames = sinogram.shape[2]
    voxel_piece = VT * tile // lax.axis_size("row")
    ray_piece = RT * tile // lax.axis_size("col")

    def ray_block_of(state):
        return state[0].astype(jnp.bfloat16)

    def voxel_total(term):
        return lax.psum(term, "row")

    residual = lax.all_gather(sinogram, "col", axis=1, tiled=True)
    volume = jnp.zeros((1, VT * tile, frames), jnp.float32)

    def backward(state):
        return voxel_total(
            backward_local(blocks, rows_index, cols_index, count, ray_block_of(state))[None]
        )

    search = backward(residual)
    gamma = lax.psum(frame_squares(search), "col")
    direction = search
    for step in range(ITERS):
        image = lax.psum(
            forward_local(blocks, rows_index, cols_index, count, direction[0].astype(jnp.bfloat16))[
                None
            ],
            "col",
        )
        alpha = gamma / lax.psum(frame_squares(image), "row")
        volume = volume + alpha * direction
        residual = residual - alpha * image
        if step + 1 < ITERS:
            search = backward(residual)
            fresh = lax.psum(frame_squares(search), "col")
            direction = search + fresh / gamma * direction
            gamma = fresh
    return (
        lax.dynamic_slice_in_dim(volume, lax.axis_index("row") * voxel_piece, voxel_piece, 1),
        lax.dynamic_slice_in_dim(residual, lax.axis_index("col") * ray_piece, ray_piece, 1),
    )


def solution(mesh):
    return jax.shard_map(
        local,
        mesh=mesh,
        in_specs=(
            P("row", "col", None, None, None),
            P("row", "col", None),
            P("row", "col", None),
            P("row", "col"),
            P("row", "col", None),
        ),
        out_specs=(P("col", "row", None), P("row", "col", None)),
        check_vma=False,
    )
```

profile of v0, /device:TPU:0, one launch (start us, length us, event | category | flops | bytes accessed | tf_op | source)
XLA Modules:
  0.0 851.2 jit_solution(9143394102961914901)
XLA Ops:
  9.9 43.2 %all-gather.2.cloned.1.call-done = f32[1,2048,128]{2,1,0:T(8,128)} async-done(((f32[1,256,128]{2,1,0:T(8,128)}), f32[1,2048,128]{2,1,0:T(8,128)}) %all-gather.2.cloned.1.call-update) | async-done | bytes 1048592 | tf_op jit(solution)/shard_map/all_gather | solution.py:59
  65.8 9.3 %copy.15 = f32[128,128,128]{1,0,2:T(8,128)} copy(f32[128,128,128]{2,1,0:T(8,128)} %fusion.30) | data formatting | bytes 16777216 | tf_op jit(solution)/shard_map/tji,tjk->tik/dot_general | solution.py:34
  81.7 35.1 %all-reduce.9.cloned.1.call-done = f32[1,2048,128]{2,1,0:T(8,128)} async-done(((f32[1,2048,128]{2,1,0:T(8,128)}), f32[1,2048,128]{2,1,0:T(8,128)}) %all-reduce.9.cloned.1.call-update) | async-done | bytes 1048592 | tf_op jit(solution)/shard_map/psum | solution.py:57
  121.8 9.9 %fusion.28 = f32[128,128,128]{2,1,0:T(8,128)} fusion(bf16[1,1,128,128,128]{4,3,2,1,0:T(8,128)(2,1)} %param.7, bf16[128,128,128]{2,1,0:T(8,128)(2,1)} %gather_fusion.1, pred[128]{0:T(512)(128)(4,1)S(1)} %get-tuple-element.15), kind=kOutput, calls=%fused_computation.36 | convolution fusion | flops 538968064 | bytes 16777344 | tf_op jit(solution)/shard_map/tij,tjk->tik/dot_general | solution.py:20
  131.7 9.3 %copy.16 = f32[128,128,128]{1,0,2:T(8,128)} copy(f32[128,128,128]{2,1,0:T(8,128)} %fusion.28) | data formatting | bytes 16777216 | tf_op jit(solution)/shard_map/tij,tjk->tik/dot_general | solution.py:20
  147.5 21.7 %psum.113 = f32[128]{0:T(128)S(1)} all-reduce(f32[128]{0:T(128)S(1)} %get-tuple-element.13), channel_id=1, replica_groups=mesh['row'=4,'col'=8] {'col'}, use_global_device_ids=true, to_apply=%region_2.4 | all-reduce | flops 128 | bytes 1024 | tf_op jit(solution)/shard_map/psum | solution.py:68
  169.2 57.2 %all-reduce.11.cloned.1.call-done = f32[1,2048,128]{2,1,0:T(8,128)} async-done(((f32[1,2048,128]{2,1,0:T(8,128)}), f32[1,2048,128]{2,1,0:T(8,128)}) %all-reduce.11.cloned.1.call-update) | async-done | bytes 1048592 | tf_op jit(solution)/shard_map/psum | solution.py:71
  247.4 9.3 %copy.17 = f32[128,128,128]{1,0,2:T(8,128)} copy(f32[128,128,128]{2,1,0:T(8,128)} %fusion.26) | data formatting | bytes 16777216 | tf_op jit(solution)/shard_map/tji,tjk->tik/dot_general | solution.py:34
  263.2 35.4 %all-reduce.13.cloned.1.call-done = f32[1,2048,128]{2,1,0:T(8,128)} async-done(((f32[1,2048,128]{2,1,0:T(8,128)}), f32[1,2048,128]{2,1,0:T(8,128)}) %all-reduce.13.cloned.1.call-update) | async-done | bytes 1048592 | tf_op jit(solution)/shard_map/psum | solution.py:57
  300.2 21.4 %psum.117 = f32[128]{0:T(128)S(1)} all-reduce(f32[128]{0:T(128)S(1)} %multiply_reduce_fusion.5), channel_id=1, replica_groups=mesh['row'=4,'col'=8] {'col'}, use_global_device_ids=true, to_apply=%region_8.10 | all-reduce | flops 128 | bytes 1024 | tf_op jit(solution)/shard_map/psum | solution.py:82
  326.9 9.9 %fusion.24 = f32[128,128,128]{2,1,0:T(8,128)} fusion(bf16[1,1,128,128,128]{4,3,2,1,0:T(8,128)(2,1)} %param.7, bf16[128,128,128]{2,1,0:T(8,128)(2,1)} %gather_fusion.3, pred[128]{0:T(512)(128)(4,1)S(1)} %get-tuple-element.15), kind=kOutput, calls=%fused_computation.32 | convolution fusion | flops 538968064 | bytes 16777344 | tf_op jit(solution)/shard_map/tij,tjk->tik/dot_general | solution.py:20
  336.8 9.3 %copy.18 = f32[128,128,128]{1,0,2:T(8,128)} copy(f32[128,128,128]{2,1,0:T(8,128)} %fusion.24) | data formatting | bytes 16777216 | tf_op jit(solution)/shard_map/tij,tjk->tik/dot_general | solution.py:20
  352.7 75.3 %all-reduce.15.cloned.1.call-done = f32[1,2048,128]{2,1,0:T(8,128)} async-done(((f32[1,2048,128]{2,1,0:T(8,128)}), f32[1,2048,128]{2,1,0:T(8,128)}) %all-reduce.15.cloned.1.call-update) | async-done | bytes 1048592 | tf_op jit(solution)/shard_map/psum | solution.py:71
  450.1 9.3 %copy.19 = f32[128,128,128]{1,0,2:T(8,128)} copy(f32[128,128,128]{2,1,0:T(8,128)} %fusion.22) | data formatting | bytes 16777216 | tf_op jit(solution)/shard_map/tji,tjk->tik/dot_general | solution.py:34
  466.0 35.4 %all-reduce.17.cloned.1.call-done = f32[1,2048,128]{2,1,0:T(8,128)} async-done(((f32[1,2048,128]{2,1,0:T(8,128)}), f32[1,2048,128]{2,1,0:T(8,128)}) %all-reduce.17.cloned.1.call-update) | async-done | bytes 1048592 | tf_op jit(solution)/shard_map/psum | solution.py:57
  502.9 21.4 %psum.121 = f32[128]{0:T(128)S(1)} all-reduce(f32[128]{0:T(128)S(1)} %multiply_reduce_fusion.3), channel_id=1, replica_groups=mesh['row'=4,'col'=8] {'col'}, use_global_device_ids=true, to_apply=%region_14.16 | all-reduce | flops 128 | bytes 1024 | tf_op jit(solution)/shard_map/psum | solution.py:82
  528.7 9.9 %fusion.20 = f32[128,128,128]{2,1,0:T(8,128)} fusion(bf16[1,1,128,128,128]{4,3,2,1,0:T(8,128)(2,1)} %param.7, bf16[128,128,128]{2,1,0:T(8,128)(2,1)} %gather_fusion.5, pred[128]{0:T(512)(128)(4,1)S(1)} %get-tuple-element.15), kind=kOutput, calls=%fused_computation.28 | convolution fusion | flops 538968064 | bytes 16777344 | tf_op jit(solution)/shard_map/tij,tjk->tik/dot_general | solution.py:20
  538.6 9.3 %copy.20 = f32[128,128,128]{1,0,2:T(8,128)} copy(f32[128,128,128]{2,1,0:T(8,128)} %fusion.20) | data formatting | bytes 16777216 | tf_op jit(solution)/shard_map/tij,tjk->tik/dot_general | solution.py:20
  554.5 75.2 %all-reduce.19.cloned.1.call-done = f32[1,2048,128]{2,1,0:T(8,128)} async-done(((f32[1,2048,128]{2,1,0:T(8,128)}), f32[1,2048,128]{2,1,0:T(8,128)}) %all-reduce.19.cloned.1.call-update) | async-done | bytes 1048592 | tf_op jit(solution)/shard_map/psum | solution.py:71
  667.9 35.4 %all-reduce.21.cloned.1.call-done = f32[1,2048,128]{2,1,0:T(8,128)} async-done(((f32[1,2048,128]{2,1,0:T(8,128)}), f32[1,2048,128]{2,1,0:T(8,128)}) %all-reduce.21.cloned.1.call-update) | async-done | bytes 1048592 | tf_op jit(solution)/shard_map/psum | solution.py:57
  704.8 21.4 %psum.125 = f32[128]{0:T(128)S(1)} all-reduce(f32[128]{0:T(128)S(1)} %multiply_reduce_fusion.1), channel_id=1, replica_groups=mesh['row'=4,'col'=8] {'col'}, use_global_device_ids=true, to_apply=%region_20.22 | all-reduce | flops 128 | bytes 1024 | tf_op jit(solution)/shard_map/psum | solution.py:82
  731.6 9.9 %fusion.16 = f32[128,128,128]{2,1,0:T(8,128)} fusion(bf16[1,1,128,128,128]{4,3,2,1,0:T(8,128)(2,1)} %param.7, bf16[128,128,128]{2,1,0:T(8,128)(2,1)} %gather_fusion.7, pred[128]{0:T(512)(128)(4,1)S(1)} %get-tuple-element.15), kind=kOutput, calls=%fused_computation.24 | convolution fusion | flops 538968064 | bytes 16777344 | tf_op jit(solution)/shard_map/tij,tjk->tik/dot_general | solution.py:20
  741.6 9.3 %copy.22 = f32[128,128,128]{1,0,2:T(8,128)} copy(f32[128,128,128]{2,1,0:T(8,128)} %fusion.16) | data formatting | bytes 16777216 | tf_op jit(solution)/shard_map/tij,tjk->tik/dot_general | solution.py:20
  757.4 75.4 %all-reduce.23.cloned.1.call-done = f32[1,2048,128]{2,1,0:T(8,128)} async-done(((f32[1,2048,128]{2,1,0:T(8,128)}), f32[1,2048,128]{2,1,0:T(8,128)}) %all-reduce.23.cloned.1.call-update) | async-done | bytes 1048592 | tf_op jit(solution)/shard_map/psum | solution.py:71
  (93 shorter events, 178.2 us)
Async XLA Ops:
  7.2 46.0 %all-gather.2.cloned.1.call-start = ((), (), s32[]{:S(2)}) async-start(), calls=%async_computation | async-start | bytes 1179648 | tf_op jit(solution)/shard_map/all_gather | solution.py:59
  7.9 108.9 %all-reduce.9.cloned.1.call-start = ((), (), s32[]{:S(2)}) async-start(), calls=%async_computation.1 | async-start | bytes 2097152 | tf_op jit(solution)/shard_map/psum | solution.py:57
  65.8 9.3 %copy-start.4 = (s32[1,1,128]{2,1,0:T(1,128)S(1)}, s32[1,1,128]{2,1,0:T(1,128)}, u32[]{:S(2)}) copy-start(s32[1,1,128]{2,1,0:T(1,128)} %param.9) | copy-start | bytes 1540
  81.7 144.7 %all-reduce.11.cloned.1.call-start = ((), (), s32[]{:S(2)}) async-start(), calls=%async_computation.2 | async-start | bytes 2097152 | tf_op jit(solution)/shard_map/psum | solution.py:71
  131.7 9.3 %copy-start.5 = (s32[1,1,128]{2,1,0:T(1,128)S(1)}, s32[1,1,128]{2,1,0:T(1,128)}, u32[]{:S(2)}) copy-start(s32[1,1,128]{2,1,0:T(1,128)} %param.8) | copy-start | bytes 1540
  146.1 88.5 %copy-start = (f32[1,2048,128]{2,1,0:T(8,128)S(1)}, f32[1,2048,128]{2,1,0:T(8,128)}, u32[]{:S(2)}) copy-start(f32[1,2048,128]{2,1,0:T(8,128)} %all-gather.2.cloned.1.call-done) | copy-start | bytes 3145732
  147.5 151.2 %all-reduce.13.cloned.1.call-start = ((), (), s32[]{:S(2)}) async-start(), calls=%async_computation.3 | async-start | bytes 2097152 | tf_op jit(solution)/shard_map/psum | solution.py:57
  261.8 59.7 %copy-start.2 = (f32[1,2048,128]{2,1,0:T(8,128)S(1)}, f32[1,2048,128]{2,1,0:T(8,128)}, u32[]{:S(2)}) copy-start(f32[1,2048,128]{2,1,0:T(8,128)} %all-reduce.9.cloned.1.call-done) | copy-start | bytes 3145732
  263.2 164.8 %all-reduce.15.cloned.1.call-start = ((), (), s32[]{:S(2)}) async-start(), calls=%async_computation.4 | async-start | bytes 2097152 | tf_op jit(solution)/shard_map/psum | solution.py:71
  351.3 85.0 %copy-start.1 = (f32[1,2048,128]{2,1,0:T(8,128)S(1)}, f32[1,2048,128]{2,1,0:T(8,128)}, u32[]{:S(2)}) copy-start(f32[1,2048,128]{2,1,0:T(8,128)} %all-reduce.11.cloned.1.call-done) | copy-start | bytes 3145732
  352.7 148.8 %all-reduce.17.cloned.1.call-start = ((), (), s32[]{:S(2)}) async-start(), calls=%async_computation.5 | async-start | bytes 2097152 | tf_op jit(solution)/shard_map/psum | solution.py:57
  464.6 59.7 %copy-start.3 = (f32[1,2048,128]{2,1,0:T(8,128)S(1)}, f32[1,2048,128]{2,1,0:T(8,128)}, u32[]{:S(2)}) copy-start(f32[1,2048,128]{2,1,0:T(8,128)} %get-tuple-element.12) | copy-start | bytes 3145732
  466.0 163.7 %all-reduce.19.cloned.1.call-start = ((), (), s32[]{:S(2)}) async-start(), calls=%async_computation.6 | async-start | bytes 2097152 | tf_op jit(solution)/shard_map/psum | solution.py:71
  554.4 148.9 %all-reduce.21.cloned.1.call-start = ((), (), s32[]{:S(2)}) async-start(), calls=%async_computation.7 | async-start | bytes 2097152 | tf_op jit(solution)/shard_map/psum | solution.py:57
  667.8 164.9 %all-reduce.23.cloned.1.call-start = ((), (), s32[]{:S(2)}) async-start(), calls=%async_computation.8 | async-start | bytes 2097152 | tf_op jit(solution)/shard_map/psum | solution.py:71
Sparse Core Ops, SparseCore 0:
  10.1 42.9 all-gather.1
  81.8 34.9 all-reduce.8
  147.6 78.7 all-reduce.10
  263.3 35.3 all-reduce.12
  352.8 75.2 all-reduce.14
  466.1 35.3 all-reduce.16
  554.6 75.0 all-reduce.18
  668.0 35.3 all-reduce.20
  757.5 75.2 all-reduce.22
where the time goes:
time: 861 us; the launch traced here: 851 us
  waiting for transfers between devices  468 us (54%)
  matrix products  114 us (13%)
  blocking collectives  112 us (13%)
  local copies, waits for them, and re-layouts  109 us (13%)
  other arithmetic  31.2 us (4%)
  between operations  15.1 us (2%)
    psum x4, waiting for transfers between devices, local(): lax.psum(forward_local(blocks, rows_index, cols_index, count, direction[0...  283 us
    psum x4, waiting for transfers between devices, voxel_total(): return lax.psum(term, 'row')  141 us
    psum x3, blocking collectives, local(): fresh = lax.psum(frame_squares(search), 'col')  64.1 us
    all_gather x1, waiting for transfers between devices, local(): residual = lax.all_gather(sinogram, 'col', axis=1, tiled=True)  43.2 us
    dot_general x4, matrix products, forward_local(): jnp.einsum('tij,tjk->tik', blocks, picked, preferred_element_type=jnp.flo...  39.7 us
    dot_general x4, local copies, waits for them, and re-layouts, forward_local(): jnp.einsum('tij,tjk->tik', blocks, picked, preferred_element_type=jnp.flo...  37.1 us
    dot_general x4, local copies, waits for them, and re-layouts, backward_local(): jnp.einsum('tji,tjk->tik', blocks, picked, preferred_element_type=jnp.flo...  37.1 us
    dot_general x4, matrix products, backward_local(): jnp.einsum('tji,tjk->tik', blocks, picked, preferred_element_type=jnp.flo...  33.5 us
  transfers between devices with their start and end apart: 9, of which 9 were waited for; matrix products, arithmetic and copies ran while one was open for 0% of the time, Pallas kernels for 0%

commit v1 on v0

v1 whole, which is shorter than its diff:
```python
import functools

import jax
import jax.numpy as jnp
from jax import lax
from jax.experimental import pallas as pl
from jax.experimental.pallas import tpu as pltpu
from jax.sharding import PartitionSpec as P

RT = 16
VT = 16
ITERS = 4
CORES = 2
MESH = pl.DeviceIdType.MESH
F32 = jnp.float32
BF16 = jnp.bfloat16


def inner_size(n):
    size = 1
    while size * 2 * size * 2 <= n and n % (size * 2) == 0:
        size *= 2
    return size


def spread_kernel(rows_ref, cols_ref, count_ref, tiles_ref, dense_ref, flipped_ref):
    tile = tiles_ref.shape[1]
    dense_ref[...] = jnp.zeros_like(dense_ref)
    flipped_ref[...] = jnp.zeros_like(flipped_ref)

    def place(t, carry):
        r = pl.multiple_of(rows_ref[t] * tile, tile)
        c = pl.multiple_of(cols_ref[t] * tile, tile)
        block = tiles_ref[t]
        dense_ref[pl.ds(r, tile), pl.ds(c, tile)] = block
        flipped_ref[pl.ds(c, tile), pl.ds(r, tile)] = block.T
        return carry

    lax.fori_loop(0, count_ref[0], place, 0)


class Axis:
    def __init__(self, name, n, n_in, chunk, refs):
        self.name, self.n, self.n_in, self.n_out, self.chunk = name, n, n_in, n // n_in, chunk
        self.near_out, self.near_in, self.far_out, self.far_in, self.norm_in = refs[:5]
        (self.near_ss, self.near_rs, self.far_ss, self.far_rs, self.out_ss, self.out_rs,
         self.in_ss, self.in_rs, self.norm_ss, self.norm_rs) = refs[5:]
        self.me = lax.axis_index(name)
        self.o, self.i = self.me // n_in, lax.rem(self.me, n_in)

    def index(self, e, d):
        return lax.rem(self.o + e + self.n_out, self.n_out) * self.n_in + lax.rem(self.i + d + self.n_in, self.n_in)

    def rows(self, index):
        return pl.ds(pl.multiple_of(index * self.chunk, self.chunk), self.chunk)

    def send(self, src, dst, ss, rs, index):
        copy = pltpu.make_async_remote_copy(
            src_ref=src, dst_ref=dst, send_sem=ss, recv_sem=rs,
            device_id={self.name: index}, device_id_type=MESH,
        )
        copy.start()
        return copy

    def outer_order(self):
        return sorted(range(1, self.n_out), key=lambda e: -min(e, self.n_out - e)) + [0]

    def reduce_scatter(self, matrix, full):
        def piece(index):
            return jnp.dot(matrix[self.rows(index), :], full[...], preferred_element_type=F32)

        copies = []
        near = {}
        for e in self.outer_order():
            for d in range(1, self.n_in):
                self.near_out[d - 1, e] = piece(self.index(e, d)).astype(BF16)
                near[e, d] = self.send(
                    self.near_out.at[d - 1, e], self.near_in.at[d - 1, e],
                    self.near_ss.at[d - 1, e], self.near_rs.at[d - 1, e], self.index(0, d))
        far = {}
        total = None
        for e in self.outer_order():
            total = piece(self.index(e, 0))
            for d in range(1, self.n_in):
                near[e, d].wait_recv()
                total += self.near_in[d - 1, e].astype(F32)
            if e:
                self.far_out[e - 1] = total.astype(BF16)
                far[e] = self.send(
                    self.far_out.at[e - 1], self.far_in.at[e - 1],
                    self.far_ss.at[e - 1], self.far_rs.at[e - 1], self.index(e, 0))
        for e in far:
            far[e].wait_recv()
            total += self.far_in[e - 1].astype(F32)
        for copy in list(near.values()) + list(far.values()):
            copy.wait_send()
        return total

    def all_gather(self, value, full):
        full[self.rows(self.me), :] = value.astype(BF16)
        mine = full.at[self.rows(self.me), :]
        far, near = {}, {}
        for e in self.outer_order()[:-1]:
            far[e] = self.send(mine, mine, self.out_ss.at[e - 1], self.out_rs.at[e - 1], self.index(e, 0))
        for d in range(1, self.n_in):
            near[0, d] = self.send(mine, mine, self.in_ss.at[d - 1, 0], self.in_rs.at[d - 1, 0], self.index(0, d))
        for e in reversed(self.outer_order()[:-1]):
            far[e].wait_recv()
            theirs = full.at[self.rows(self.index(-e, 0)), :]
            for d in range(1, self.n_in):
                near[e, d] = self.send(
                    theirs, theirs, self.in_ss.at[d - 1, e], self.in_rs.at[d - 1, e], self.index(0, d))
        for copy in near.values():
            copy.wait_recv()
        for copy in list(near.values()) + list(far.values()):
            copy.wait_send()

    def peer(self, d):
        return lax.rem(self.me + d, self.n)

    def norm_send(self, value, which):
        self.norm_in[which, 0] = jnp.broadcast_to(value, self.norm_in.shape[2:])
        return [
            self.send(self.norm_in.at[which, 0], self.norm_in.at[which, d],
                      self.norm_ss.at[which, d - 1], self.norm_rs.at[which, d - 1], self.peer(d))
            for d in range(1, self.n)
        ]

    def norm_wait(self, which):
        for d in range(1, self.n):
            pltpu.make_async_remote_copy(
                src_ref=self.norm_in.at[which, 0], dst_ref=self.norm_in.at[which, d],
                send_sem=self.norm_ss.at[which, d - 1], recv_sem=self.norm_rs.at[which, d - 1],
                device_id={self.name: self.peer(d)}, device_id_type=MESH,
            ).wait()
        total = self.norm_in[which, 0]
        for d in range(1, self.n):
            total += self.norm_in[which, d]
        return total[0:1, :]


def squares(ref, step):
    total = None
    for at in range(0, ref.shape[0], step):
        part = ref[at:at + step, :].astype(F32)
        part = jnp.sum(part * part, axis=0, keepdims=True)
        total = part if total is None else total + part
    return total


def cgls_kernel(sizes, dense_hbm, flipped_hbm, sino_ref, volume_ref, residual_ref, dense, flipped, rays, voxels,
                search, direction, image, gamma, load_sem, *refs):
    n_row, n_col, col_in = sizes
    half = len(refs) // 2
    row = Axis("row", n_row, CORES, search.shape[0], refs[:half])
    col = Axis("col", n_col, col_in, image.shape[0], refs[half:])

    loads = [
        pltpu.make_async_copy(flipped_hbm, flipped, load_sem.at[0]),
        pltpu.make_async_copy(dense_hbm, dense, load_sem.at[1]),
    ]
    for load in loads:
        load.start()

    barrier = pltpu.get_barrier_semaphore()
    for axis in (row, col):
        for d in range(1, axis.n):
            pl.semaphore_signal(barrier, inc=1, device_id={axis.name: axis.peer(d)}, device_id_type=MESH)
    pl.semaphore_wait(barrier, n_row + n_col - 2)

    col.all_gather(sino_ref[...], rays)
    residual_ref[...] = sino_ref[...]
    volume_ref[...] = jnp.zeros_like(volume_ref)
    direction[...] = jnp.zeros_like(direction)
    image[...] = jnp.zeros_like(image)
    gamma[...] = jnp.ones_like(gamma)
    for load in loads:
        load.wait()

    def iteration(k, carry):
        search[...] = row.reduce_scatter(flipped, rays)
        row.all_gather(search[...], voxels)
        col.norm_send(squares(voxels, 256), 0)
        forth = col.reduce_scatter(dense, voxels)
        fresh = col.norm_wait(0)
        beta = jnp.where(k > 0, fresh / gamma[...], jnp.zeros_like(fresh))
        gamma[...] = fresh
        image[...] = forth + beta * image[...]
        col.norm_send(squares(image, image.shape[0]), 1)
        direction[...] = search[...] + beta * direction[...]
        row.norm_send(col.norm_wait(1), 0)
        alpha = fresh / row.norm_wait(0)
        residual_ref[...] -= alpha * image[...]

        @pl.when(k + 1 < ITERS)
        def _():
            col.all_gather(residual_ref[...], rays)

        volume_ref[...] += alpha * direction[...]
        return carry

    lax.fori_loop(0, ITERS, iteration, 0)


def axis_scratch(n, n_in, chunk, frames):
    n_out = n // n_in
    dma = pltpu.SemaphoreType.DMA
    near, far = (max(n_in - 1, 1), n_out), (max(n_out - 1, 1),)
    return [
        pltpu.VMEM(near + (chunk, frames), BF16),
        pltpu.VMEM(near + (chunk, frames), BF16),
        pltpu.VMEM(far + (chunk, frames), BF16),
        pltpu.VMEM(far + (chunk, frames), BF16),
        pltpu.VMEM((2, n, 8, frames), F32),
        dma(near), dma(near), dma(far), dma(far), dma(far), dma(far), dma(near), dma(near),
        dma((2, n - 1)), dma((2, n - 1)),
    ]


def local(n_row, n_col, tiles, tile_row, tile_col, tile_count, sinogram):
    tile, frames = tiles.shape[3], sinogram.shape[2]
    n_rays, n_vox = RT * tile, VT * tile
    vmem = pl.BlockSpec(memory_space=pltpu.VMEM)
    smem = pl.BlockSpec(memory_space=pltpu.SMEM)
    dense, flipped = pl.pallas_call(
        spread_kernel,
        out_shape=(
            jax.ShapeDtypeStruct((n_rays, n_vox), BF16),
            jax.ShapeDtypeStruct((n_vox, n_rays), BF16),
        ),
        in_specs=[smem, smem, smem, vmem],
        out_specs=(vmem, vmem),
        compiler_params=pltpu.CompilerParams(vmem_limit_bytes=40 * 1024 * 1024),
        name="spread",
    )(tile_row[0, 0], tile_col[0, 0], tile_count[0], tiles[0, 0])

    col_in = inner_size(n_col)
    vox_piece, ray_piece = n_vox // n_row, n_rays // n_col
    hbm = pl.BlockSpec(memory_space=pl.ANY)
    volume, residual = pl.pallas_call(
        functools.partial(cgls_kernel, (n_row, n_col, col_in)),
        out_shape=(
            jax.ShapeDtypeStruct((vox_piece, frames), F32),
            jax.ShapeDtypeStruct((ray_piece, frames), F32),
        ),
        in_specs=[hbm, hbm, vmem],
        out_specs=(vmem, vmem),
        scratch_shapes=[
            pltpu.VMEM((n_rays, n_vox), BF16),
            pltpu.VMEM((n_vox, n_rays), BF16),
            pltpu.VMEM((n_rays, frames), BF16),
            pltpu.VMEM((n_vox, frames), BF16),
            pltpu.VMEM((vox_piece, frames), F32),
            pltpu.VMEM((vox_piece, frames), F32),
            pltpu.VMEM((ray_piece, frames), F32),
            pltpu.VMEM((1, frames), F32),
            pltpu.SemaphoreType.DMA((2,)),
        ]
        + axis_scratch(n_row, CORES, vox_piece, frames)
        + axis_scratch(n_col, col_in, ray_piece, frames),
        compiler_params=pltpu.CompilerParams(
            collective_id=0, has_side_effects=True, vmem_limit_bytes=40 * 1024 * 1024
        ),
        name="cgls",
    )(dense, flipped, sinogram[0])
    return volume[None], residual[None]


def solution(mesh):
    return jax.shard_map(
        functools.partial(local, mesh.shape["row"], mesh.shape["col"]),
        mesh=mesh,
        in_specs=(
            P("row", "col", None, None, None),
            P("row", "col", None),
            P("row", "col", None),
            P("row", "col"),
            P("row", "col", None),
        ),
        out_specs=(P("col", "row", None), P("row", "col", None)),
        check_vma=False,
    )
```

time: 861 us -> 204 us (0.24); the launches traced: 851 us -> 204 us
  waiting for transfers between devices: 468 us -> 0 us
  Pallas kernels: 0 us -> 197 us
  matrix products: 114 us -> 0 us
  blocking collectives: 112 us -> 0 us
  local copies, waits for them, and re-layouts: 109 us -> 5.75 us
  other arithmetic: 31.2 us -> 0 us
  between operations: 15.1 us -> 1.3 us
    psum x8 -> x0, waiting for transfers between devices: 424 us -> none  [the longest x4 283 us: local(): lax.psum(forward_local(blocks, rows_index, cols_index, count, direction[0...]
    pallas_call x0 -> x2, Pallas kernels: none -> 197 us  [the longest x1 191 us: local(): pl.pallas_call(functools.partial(cgls_kernel, (n_row, n_col, col_in)), ou...]
    dot_general x16 -> x0, matrix products: 114 us -> none  [the longest x4 39.7 us: forward_local(): jnp.einsum('tij,tjk->tik', blocks, picked, preferred_element_type=jnp.flo...]
    psum x8 -> x0, blocking collectives: 112 us -> none  [the longest x3 64.1 us: local(): fresh = lax.psum(frame_squares(search), 'col')]
    dot_general x16 -> x0, local copies, waits for them, and re-layouts: 84.9 us -> none  [the longest x4 37.1 us: forward_local(): jnp.einsum('tij,tjk->tik', blocks, picked, preferred_element_type=jnp.flo...]
    all_gather x1 -> x0, waiting for transfers between devices: 43.2 us -> none  [local(): residual = lax.all_gather(sinogram, 'col', axis=1, tiled=True)]
    gather x8 -> x0, local copies, waits for them, and re-layouts: 24.5 us -> none  [the longest x4 12.2 us: backward_local(): picked = jnp.take(ray_tiles, rows_index, axis=0)]
    convert_element_type x7 -> x0, other arithmetic: 13.9 us -> none  [the longest x4 7.75 us: ray_block_of(): return state[0].astype(jnp.bfloat16)]
  transfers between devices with their start and end apart: 9 -> 0, of which waited for: 9 -> 0; matrix products, arithmetic and copies ran while one was open for 0% -> 0% of each run, Pallas kernels for 0% -> 0%
where the time goes in v1:
time: 204 us
  Pallas kernels  197 us (97%)
  local copies, waits for them, and re-layouts  5.75 us (3%)
    pallas_call x1, Pallas kernels, local(): pl.pallas_call(functools.partial(cgls_kernel, (n_row, n_col, col_in)), ou...  191 us
    pallas_call x1, Pallas kernels, local(): pl.pallas_call(spread_kernel, out_shape=(jax.ShapeDtypeStruct((n_rays, n_...  6.61 us
    unnamed x10, local copies, waits for them, and re-layouts  5.75 us

profile of v1, /device:TPU:0, one launch (start us, length us, event | category | flops | bytes accessed | tf_op | source)
XLA Modules:
  0.0 204.5 jit_solution(18329595141427626245)
XLA Ops:
  1.3 0.0 copy-start
  1.3 2.2 %copy-done = bf16[1,1,128,128,128]{4,3,2,1,0:T(8,128)(2,1)S(1)} copy-done((bf16[1,1,128,128,128]{4,3,2,1,0:T(8,128)(2,1)S(1)}, bf16[1,1,128,128,128]{4,3,2,1,0:T(8,128)(2,1)}, u32[]{:S(2)}) %copy-start) | copy-done | bytes 4194328
  3.5 0.0 copy-start.2
  3.5 0.7 copy-done.2
  4.1 0.0 copy-start.3
  4.1 0.7 copy-done.3
  4.8 6.6 %spread.1 = (bf16[2048,2048]{1,0:T(8,128)(2,1)S(1)}, bf16[2048,2048]{1,0:T(8,128)(2,1)}) custom-call(s32[128]{0:T(128)S(1)} %bitcast.12, s32[128]{0:T(128)S(1)} %bitcast.13, s32[1]{0:T(128)} %bitcast.7.count_ref, bf16[128,128,128]{2,1,0:T(8,128)(2,1)S(1)} %bitcast.8), custom_call_target="tpu_custom_call" | custom-call | tf_op jit(solution)/shard_map/spread/pallas_call | solution.py:225
  11.4 0.0 copy-start.1
  11.4 0.9 copy-done.1
  12.3 190.8 %cgls.1 = (f32[512,128]{1,0:T(8,128)S(1)}, f32[256,128]{1,0:T(8,128)S(1)}) custom-call(bf16[2048,2048]{1,0:T(8,128)(2,1)S(1)} %get-tuple-element.6.dense_hbm, bf16[2048,2048]{1,0:T(8,128)(2,1)} %get-tuple-element.7.flipped_hbm, f32[256,128]{1,0:T(8,128)S(1)} %bitcast.10), custom_call_target="tpu_custom_call" | custom-call | tf_op jit(solution)/shard_map/cgls/pallas_call | solution.py:240
  203.1 0.7 copy.10
  203.8 0.7 copy.11
Async XLA Ops:
  1.3 2.2 %copy-start = (bf16[1,1,128,128,128]{4,3,2,1,0:T(8,128)(2,1)S(1)}, bf16[1,1,128,128,128]{4,3,2,1,0:T(8,128)(2,1)}, u32[]{:S(2)}) copy-start(bf16[1,1,128,128,128]{4,3,2,1,0:T(8,128)(2,1)} %param.5) | copy-start | bytes 12582916
  3.5 0.7 copy-start.2
  4.1 0.7 copy-start.3
  11.4 0.9 copy-start.1

commit v2 on v1

--- a/solution.py
+++ b/solution.py
@@ -23,20 +23,21 @@
     return size
 
 
-def spread_kernel(rows_ref, cols_ref, count_ref, tiles_ref, dense_ref, flipped_ref):
-    tile = tiles_ref.shape[1]
-    dense_ref[...] = jnp.zeros_like(dense_ref)
-    flipped_ref[...] = jnp.zeros_like(flipped_ref)
-
-    def place(t, carry):
-        r = pl.multiple_of(rows_ref[t] * tile, tile)
-        c = pl.multiple_of(cols_ref[t] * tile, tile)
-        block = tiles_ref[t]
-        dense_ref[pl.ds(r, tile), pl.ds(c, tile)] = block
-        flipped_ref[pl.ds(c, tile), pl.ds(r, tile)] = block.T
+def build(slot_ref, tiles, dense, flipped, start, stop):
+    tile = tiles.shape[1]
+    group = 4
+
+    def place(step, carry):
+        for j in range(group):
+            at = step * group + j
+            r = pl.multiple_of(at // VT * tile, tile)
+            c = pl.multiple_of(lax.rem(at, VT) * tile, tile)
+            block = tiles[slot_ref[at]]
+            dense[pl.ds(r, tile), pl.ds(c, tile)] = block
+            flipped[pl.ds(c, tile), pl.ds(r, tile)] = block.T
         return carry
 
-    lax.fori_loop(0, count_ref[0], place, 0)
+    lax.fori_loop(start // group, stop // group, place, 0)
 
 
 class Axis:
@@ -96,7 +97,7 @@
             copy.wait_send()
         return total
 
-    def all_gather(self, value, full):
+    def all_gather(self, value, full, between=lambda step: None):
         full[self.rows(self.me), :] = value.astype(BF16)
         mine = full.at[self.rows(self.me), :]
         far, near = {}, {}
@@ -104,12 +105,14 @@
             far[e] = self.send(mine, mine, self.out_ss.at[e - 1], self.out_rs.at[e - 1], self.index(e, 0))
         for d in range(1, self.n_in):
             near[0, d] = self.send(mine, mine, self.in_ss.at[d - 1, 0], self.in_rs.at[d - 1, 0], self.index(0, d))
-        for e in reversed(self.outer_order()[:-1]):
+        between(0)
+        for step, e in enumerate(reversed(self.outer_order()[:-1])):
             far[e].wait_recv()
             theirs = full.at[self.rows(self.index(-e, 0)), :]
             for d in range(1, self.n_in):
                 near[e, d] = self.send(
                     theirs, theirs, self.in_ss.at[d - 1, e], self.in_rs.at[d - 1, e], self.index(0, d))
+            between(step + 1)
         for copy in near.values():
             copy.wait_recv()
         for copy in list(near.values()) + list(far.values()):
@@ -148,19 +151,17 @@
     return total
 
 
-def cgls_kernel(sizes, dense_hbm, flipped_hbm, sino_ref, volume_ref, residual_ref, dense, flipped, rays, voxels,
-                search, direction, image, gamma, load_sem, *refs):
+def cgls_kernel(sizes, slot_ref, tiles_hbm, sino_ref, volume_ref, residual_ref, tiles, dense, flipped, rays, voxels,
+                images, held, search, direction, image, gamma, per_alpha, load_sem, *refs):
     n_row, n_col, col_in = sizes
     half = len(refs) // 2
     row = Axis("row", n_row, CORES, search.shape[0], refs[:half])
     col = Axis("col", n_col, col_in, image.shape[0], refs[half:])
 
-    loads = [
-        pltpu.make_async_copy(flipped_hbm, flipped, load_sem.at[0]),
-        pltpu.make_async_copy(dense_hbm, dense, load_sem.at[1]),
-    ]
-    for load in loads:
-        load.start()
+    slots = tiles_hbm.shape[0]
+    load = pltpu.make_async_copy(tiles_hbm, tiles.at[pl.ds(0, slots)], load_sem)
+    load.start()
+    tiles[slots] = jnp.zeros(tiles.shape[1:], tiles.dtype)
 
     barrier = pltpu.get_barrier_semaphore()
     for axis in (row, col):
@@ -168,14 +169,21 @@
             pl.semaphore_signal(barrier, inc=1, device_id={axis.name: axis.peer(d)}, device_id_type=MESH)
     pl.semaphore_wait(barrier, n_row + n_col - 2)
 
-    col.all_gather(sino_ref[...], rays)
+    share = RT * VT // col.n_out
+
+    def build_share(step):
+        if step == 0:
+            load.wait()
+        build(slot_ref, tiles, dense, flipped, step * share, (step + 1) * share)
+
+    col.all_gather(sino_ref[...], rays, build_share)
+    held[...] = rays[...].astype(F32)
     residual_ref[...] = sino_ref[...]
     volume_ref[...] = jnp.zeros_like(volume_ref)
     direction[...] = jnp.zeros_like(direction)
     image[...] = jnp.zeros_like(image)
     gamma[...] = jnp.ones_like(gamma)
-    for load in loads:
-        load.wait()
+    per_alpha[...] = jnp.zeros_like(per_alpha)
 
     def iteration(k, carry):
         search[...] = row.reduce_scatter(flipped, rays)
@@ -187,15 +195,31 @@
         gamma[...] = fresh
         image[...] = forth + beta * image[...]
         col.norm_send(squares(image, image.shape[0]), 1)
-        direction[...] = search[...] + beta * direction[...]
-        row.norm_send(col.norm_wait(1), 0)
-        alpha = fresh / row.norm_wait(0)
-        residual_ref[...] -= alpha * image[...]
 
         @pl.when(k + 1 < ITERS)
         def _():
-            col.all_gather(residual_ref[...], rays)
-
+            def norm_on(step):
+                if step == col.n_out - 1:
+                    row.norm_send(col.norm_wait(1), 0)
+
+            drift = held[col.rows(col.me), :] - residual_ref[...]
+            col.all_gather(image[...] + drift * per_alpha[...], images, norm_on)
+
+        @pl.when(k + 1 == ITERS)
+        def _():
+            row.norm_send(col.norm_wait(1), 0)
+
+        direction[...] = search[...] + beta * direction[...]
+        energy = row.norm_wait(0)
+        alpha = fresh / energy
+        per_alpha[...] = energy / fresh
+
+        @pl.when(k + 1 < ITERS)
+        def _():
+            held[...] -= alpha * images[...].astype(F32)
+            rays[...] = held[...].astype(BF16)
+
+        residual_ref[...] -= alpha * image[...]
         volume_ref[...] += alpha * direction[...]
         return carry
 
@@ -222,17 +246,11 @@
     n_rays, n_vox = RT * tile, VT * tile
     vmem = pl.BlockSpec(memory_space=pltpu.VMEM)
     smem = pl.BlockSpec(memory_space=pltpu.SMEM)
-    dense, flipped = pl.pallas_call(
-        spread_kernel,
-        out_shape=(
-            jax.ShapeDtypeStruct((n_rays, n_vox), BF16),
-            jax.ShapeDtypeStruct((n_vox, n_rays), BF16),
-        ),
-        in_specs=[smem, smem, smem, vmem],
-        out_specs=(vmem, vmem),
-        compiler_params=pltpu.CompilerParams(vmem_limit_bytes=40 * 1024 * 1024),
-        name="spread",
-    )(tile_row[0, 0], tile_col[0, 0], tile_count[0], tiles[0, 0])
+    slots = tiles.shape[2]
+    slot = jnp.arange(slots, dtype=jnp.int32)
+    place = tile_row[0, 0] * VT + tile_col[0, 0]
+    match = (place[None, :] == jnp.arange(RT * VT, dtype=jnp.int32)[:, None]) & (slot[None, :] < tile_count[0, 0])
+    slot_of = jnp.min(jnp.where(match, slot[None, :], slots), axis=1)
 
     col_in = inner_size(n_col)
     vox_piece, ray_piece = n_vox // n_row, n_rays // n_col
@@ -243,26 +261,30 @@
             jax.ShapeDtypeStruct((vox_piece, frames), F32),
             jax.ShapeDtypeStruct((ray_piece, frames), F32),
         ),
-        in_specs=[hbm, hbm, vmem],
+        in_specs=[smem, hbm, vmem],
         out_specs=(vmem, vmem),
         scratch_shapes=[
+            pltpu.VMEM((slots + 1, tile, tile), BF16),
             pltpu.VMEM((n_rays, n_vox), BF16),
             pltpu.VMEM((n_vox, n_rays), BF16),
             pltpu.VMEM((n_rays, frames), BF16),
             pltpu.VMEM((n_vox, frames), BF16),
+            pltpu.VMEM((n_rays, frames), BF16),
+            pltpu.VMEM((n_rays, frames), F32),
             pltpu.VMEM((vox_piece, frames), F32),
             pltpu.VMEM((vox_piece, frames), F32),
             pltpu.VMEM((ray_piece, frames), F32),
             pltpu.VMEM((1, frames), F32),
-            pltpu.SemaphoreType.DMA((2,)),
+            pltpu.VMEM((1, frames), F32),
+            pltpu.SemaphoreType.DMA,
         ]
         + axis_scratch(n_row, CORES, vox_piece, frames)
         + axis_scratch(n_col, col_in, ray_piece, frames),
         compiler_params=pltpu.CompilerParams(
-            collective_id=0, has_side_effects=True, vmem_limit_bytes=40 * 1024 * 1024
+            collective_id=0, has_side_effects=True, vmem_limit_bytes=62 * 1024 * 1024
         ),
         name="cgls",
-    )(dense, flipped, sinogram[0])
+    )(slot_of, tiles[0, 0], sinogram[0])
     return volume[None], residual[None]
 
 

time: 204 us -> 174 us (0.85)
  Pallas kernels: 197 us -> 168 us
  local copies, waits for them, and re-layouts: 5.75 us -> 3.24 us
    pallas_call x1, Pallas kernels: 191 us -> 168 us  [local(): pl.pallas_call(functools.partial(cgls_kernel, (n_row, n_col, col_in)), ou...]
    pallas_call x1 -> x0, Pallas kernels: 6.61 us -> none  [local(): pl.pallas_call(spread_kernel, out_shape=(jax.ShapeDtypeStruct((n_rays, n_...]
    unnamed x10 -> x2, local copies, waits for them, and re-layouts: 5.75 us -> 3.24 us
where the time goes in v2:
time: 174 us
  Pallas kernels  168 us (97%)
  local copies, waits for them, and re-layouts  3.24 us (2%)
    pallas_call x1, Pallas kernels, local(): pl.pallas_call(functools.partial(cgls_kernel, (n_row, n_col, col_in)), ou...  168 us

profile of v2, /device:TPU:0, one launch (start us, length us, event | category | flops | bytes accessed | tf_op | source)
XLA Modules:
  0.0 173.7 jit_solution(2283252234799456635)
XLA Ops:
  1.3 0.7 add_bitcast_fusion
  2.0 0.7 select_reduce_fusion.slot_ref
  2.6 167.8 %cgls.1 = (f32[512,128]{1,0:T(8,128)}, f32[256,128]{1,0:T(8,128)}) custom-call(s32[256]{0:T(256)} %select_reduce_fusion.slot_ref, bf16[128,128,128]{2,1,0:T(8,128)(2,1)} %bitcast.8, f32[256,128]{1,0:T(8,128)} %bitcast.10), custom_call_target="tpu_custom_call" | custom-call | tf_op jit(solution)/shard_map/cgls/pallas_call | solution.py:258
  170.4 1.7 copy.10
  172.1 1.6 copy.11
  (1 shorter events, 0.0 us)
